TPU v7x, 16 devices: a 4x2x1 block of a 4x4x8 slice. The times are simulated.
16 devices in a mesh: dp: 2 (over y, z), ep: 8 (over x, core).
Axes of the slice: x: 4, y: 2, z: 1, core: 2. Of those that a mesh axis runs over, the one named last changes fastest.
The devices are a block of a 4x4x8 slice.
Arguments:
- x_tok: bfloat16 [16, 1024, 2048], P(('dp', 'ep')), parts along dimension 0
- w_query: bfloat16 [2048, 32, 128], P('ep')
- w_key: bfloat16 [2048, 32, 128], P('ep')
- w_value: bfloat16 [2048, 32, 128], P('ep')
- w_out: bfloat16 [4096, 2048], P('ep')
- w_router: float32 [2048, 128], replicated
- w_gate: bfloat16 [128, 2048, 768], P('ep')
- w_up: bfloat16 [128, 2048, 768], P('ep')
- w_down: bfloat16 [128, 768, 2048], P('ep')
- ws_gate: bfloat16 [2048, 768], P('ep')
- ws_up: bfloat16 [2048, 768], P('ep')
- ws_down: bfloat16 [768, 2048], P('ep')
- expert_ids: int32 [16, 1024, 8], P(('dp', 'ep')), parts along dimension 0
Outputs:
- output: bfloat16 [16, 1024, 2048], P(('dp', 'ep')), parts along dimension 0
There are 2 independent parts. A program takes and returns all parts, laid end to end along the dimension named above; an argument that names none is the same for every part.
All inputs are finite; a program needn't handle non-finite values.
Results may differ from a plain program's by a relative error of at most 0.0127758.
Values are sent between devices in bfloat16 or wider.
A program may use at most 768 MiB of HBM per device.

v0:
```python
import functools
import jax
import jax.numpy as jnp
from jax import lax
from jax.sharding import PartitionSpec as P

EPSILON = 1e-6
CAP_FACTOR = 2


def rms_norm(values):
    as_f32 = values.astype(jnp.float32)
    return as_f32 * lax.rsqrt(jnp.mean(as_f32 * as_f32, axis=-1, keepdims=True) + EPSILON)


def swiglu_rows(row_block, gate_w, up_w, down_w):
    gate_act = jnp.einsum('...d,df->...f', row_block, gate_w, preferred_element_type=jnp.float32)
    up_act = jnp.einsum('...d,df->...f', row_block, up_w, preferred_element_type=jnp.float32)
    middle = (jax.nn.silu(gate_act) * up_act).astype(jnp.bfloat16)
    return jnp.einsum('...f,fd->...d', middle, down_w, preferred_element_type=jnp.float32).astype(jnp.bfloat16)


def slot_plan(flat_ids, n_experts, capacity, top_k):
    n_assign = flat_ids.shape[0]
    sort_order = jnp.argsort(flat_ids, stable=True)
    expert_counts = jnp.bincount(flat_ids, length=n_experts)
    expert_starts = jnp.cumsum(expert_counts) - expert_counts
    slot_rows = jnp.minimum(expert_starts[:, None] + jnp.arange(capacity)[None, :], n_assign - 1)
    slot_token = jnp.take(sort_order, slot_rows.reshape(-1)) // top_k
    rank_of = jnp.argsort(sort_order)
    slot_of_assign = flat_ids * capacity + rank_of - jnp.take(expert_starts, flat_ids)
    return slot_token, slot_of_assign


def attention_block(x_loc, query_w, key_w, value_w, out_w):
    n_seq, seq_len, d_model = x_loc.shape
    head_dim = query_w.shape[2]
    normed = rms_norm(x_loc).astype(jnp.bfloat16)
    queries = jnp.einsum('bsd,dhe->bshe', normed, query_w, preferred_element_type=jnp.float32).astype(jnp.bfloat16)
    keys_all = jnp.einsum('bsd,dhe->bshe', normed, key_w, preferred_element_type=jnp.float32).astype(jnp.bfloat16)
    vals_all = jnp.einsum('bsd,dhe->bshe', normed, value_w, preferred_element_type=jnp.float32).astype(jnp.bfloat16)
    scores = jnp.einsum('bqhe,bkhe->bhqk', queries, keys_all, preferred_element_type=jnp.float32) * (head_dim ** -0.5)
    causal = jnp.arange(seq_len)[:, None] >= jnp.arange(seq_len)[None, :]
    attn_probs = jax.nn.softmax(jnp.where(causal, scores, -1e30), axis=-1).astype(jnp.bfloat16)
    attended = jnp.einsum('bhqk,bkhe->bqhe', attn_probs, vals_all, preferred_element_type=jnp.float32).astype(jnp.bfloat16)
    attn_out = jnp.einsum('crx,xe->cre', attended.reshape(n_seq, seq_len, -1), out_w, preferred_element_type=jnp.float32).astype(jnp.bfloat16)
    return (x_loc.astype(jnp.float32) + attn_out.astype(jnp.float32)).astype(jnp.bfloat16)


def local_layer(x_loc, q_shard, k_shard, v_shard, o_shard, w_router, gate_loc, up_loc, down_loc, sgate_shard, sup_shard, sdown_shard, ids_loc, group):
    query_w = lax.all_gather(q_shard, 'ep', axis=0, tiled=True)
    key_w = lax.all_gather(k_shard, 'ep', axis=0, tiled=True)
    value_w = lax.all_gather(v_shard, 'ep', axis=0, tiled=True)
    out_w = lax.all_gather(o_shard, 'ep', axis=0, tiled=True)
    residual = attention_block(x_loc, query_w, key_w, value_w, out_w)
    n_seq, seq_len, d_model = x_loc.shape
    n_tok = n_seq * seq_len
    top_k = ids_loc.shape[-1]
    local_experts = gate_loc.shape[0]
    n_experts = local_experts * group
    capacity = CAP_FACTOR * n_tok * top_k // n_experts
    hidden = rms_norm(residual).reshape(n_tok, d_model)
    tok_ids = ids_loc.reshape(n_tok, top_k)
    logits = jnp.dot(hidden, w_router, precision=lax.Precision.HIGHEST, preferred_element_type=jnp.float32)
    gate_probs = jax.nn.softmax(jnp.take_along_axis(logits, tok_ids, axis=1), axis=-1)
    moe_in = hidden.astype(jnp.bfloat16)
    slot_token, slot_of_assign = slot_plan(tok_ids.reshape(-1), n_experts, capacity, top_k)
    send_buf = jnp.take(moe_in, slot_token, axis=0).reshape(group, local_experts, capacity, d_model)
    received = lax.all_to_all(send_buf, 'ep', 0, 2, tiled=True).reshape(local_experts, group * capacity, d_model)
    gate_act = jnp.einsum('ecd,edf->ecf', received, gate_loc, preferred_element_type=jnp.float32)
    up_act = jnp.einsum('ecd,edf->ecf', received, up_loc, preferred_element_type=jnp.float32)
    middle = (jax.nn.silu(gate_act) * up_act).astype(jnp.bfloat16)
    expert_out = jnp.einsum('ecf,efd->ecd', middle, down_loc, preferred_element_type=jnp.float32).astype(jnp.bfloat16)
    returned = lax.all_to_all(expert_out.reshape(1, local_experts, group * capacity, d_model), 'ep', 2, 0, tiled=True)
    picked_rows = jnp.take(returned.reshape(n_experts * capacity, d_model), slot_of_assign, axis=0).reshape(n_tok, top_k, d_model)
    routed = jnp.sum(picked_rows.astype(jnp.float32) * gate_probs[:, :, None], axis=1)
    shared_gate = lax.all_gather(sgate_shard, 'ep', axis=0, tiled=True)
    shared_up = lax.all_gather(sup_shard, 'ep', axis=0, tiled=True)
    shared_down = lax.all_gather(sdown_shard, 'ep', axis=0, tiled=True)
    shared = swiglu_rows(moe_in, shared_gate, shared_up, shared_down)
    y_out = (residual.reshape(n_tok, d_model).astype(jnp.float32) + routed + shared.astype(jnp.float32)).astype(jnp.bfloat16)
    return y_out.reshape(n_seq, seq_len, d_model)


def solution(mesh):
    tok_spec = P(('dp', 'ep'), None, None)
    row_spec = P('ep', None)
    cube_spec = P('ep', None, None)
    in_specs = (tok_spec, cube_spec, cube_spec, cube_spec, row_spec, P(None, None), cube_spec, cube_spec, cube_spec, row_spec, row_spec, row_spec, tok_spec)
    return jax.shard_map(functools.partial(local_layer, group=mesh.shape['ep']), mesh=mesh, in_specs=in_specs, out_specs=tok_spec, check_vma=False)
```

profile of v0, /device:TPU:112, one launch (start us, length us, event | category | flops | bytes accessed | tf_op | source)
XLA Modules:
  0.0 2717.6 jit_solution(13762930148250089753)
XLA Ops:
  11.3 57.0 %scatter_custom_fusion = s32[128]{0:T(128)S(1)} fusion(s32[8192]{0:T(1024)S(1)} %bitcast.108, s32[8192]{0:T(1024)S(1)} %broadcast.366, s32[]{:T(128)} %constant.102.clone.1), kind=kCustom, calls=%fused_computation.96 | custom fusion | flops 8192 | bytes 516 | tf_op jit(solution)/shard_map/scatter-add | solution.py:26
  78.9 90.7 %gather_fusion.1 = s32[16384]{0:T(1024)S(1)} fusion(s32[8192]{0:T(1024)S(1)} %get-tuple-element.7, s32[16384]{0:T(1024)S(1)} %broadcast_clamp_fusion.1), kind=kCustom, calls=%fused_computation.1 | custom fusion | bytes 196608 | tf_op jit(solution)/shard_map/jit(_take)/gather | solution.py:29
  171.4 23.0 fusion.31
  194.5 23.0 fusion.34
  217.5 42.0 %all-gather.8.cloned.1.call-done = bf16[2048,32,128]{2,1,0:T(8,128)(2,1)} async-done(((bf16[256,32,128]{2,1,0:T(8,128)(2,1)}), bf16[2048,32,128]{2,1,0:T(8,128)(2,1)}) %all-gather.8.cloned.1.call-update) | async-done | bytes 16777232 | tf_op jit(solution)/shard_map/all_gather | solution.py:53
  259.5 23.4 fusion.109
  282.8 57.2 %fusion.69 = (f32[32,1024]{1,0:T(8,128)S(1)}, f32[32,1024,1024]{1,2,0:T(8,128)}) fusion(pred[1024,1024]{0,1:T(8,128)(4,1)S(1)} %iota_compare_fusion, bf16[1024,32,128]{2,0,1:T(8,128)(2,1)} %fusion.31, bf16[1024,32,128]{2,0,1:T(8,128)(2,1)} %fusion.34), kind=kOutput, calls=%fused_computation.103 | convolution fusion | flops 8724153344 | bytes 152174592 | tf_op jit(solution)/shard_map/sub | solution.py:44
  340.1 47.5 %fusion.37 = bf16[32,128,1024]{2,1,0:T(8,128)(2,1)} fusion(f32[32,1024,1024]{1,2,0:T(8,128)} %get-tuple-element.14, f32[32,1024]{1,0:T(8,128)S(1)} %get-tuple-element.13, bf16[1024,32,128]{2,0,1:T(8,128)(2,1)} %fusion.109), kind=kOutput, calls=%fused_computation.47 | convolution fusion | flops 8661237760 | bytes 151126016 | tf_op jit(solution)/shard_map/bhqk,bkhe->bqhe/dot_general | solution.py:45
  387.6 23.8 fusion.21
  416.2 124.1 %gather_fusion.2 = bf16[16384,2048]{1,0:T(8,128)(2,1)} fusion(bf16[1024,2048]{1,0:T(8,128)(2,1)} %fusion.25, s32[16384]{0:T(1024)S(1)} %copy-done.11), kind=kCustom, calls=%fused_computation.2 | custom fusion | bytes 134283264 | tf_op jit(solution)/shard_map/jit(_take)/gather | solution.py:68
  540.3 44.1 %broadcast_select_fusion = bf16[8,16,128,2048]{3,2,1,0:T(8,128)(2,1)} fusion(bf16[8,16,128,2048]{3,2,1,0:T(8,128)(2,1)} %bitcast.16, pred[8,16,128]{2,1,0:T(8,128)(4,1)S(1)} %copy-done.16), kind=kLoop, calls=%fused_computation.15 | loop fusion | flops 33554432 | bytes 134234112 | tf_op jit(solution)/shard_map/jit(_take)/select_n | solution.py:68
  584.4 741.9 %all_to_all.30 = bf16[8,16,128,2048]{3,2,1,0:T(8,128)(2,1)} all-to-all(bf16[8,16,128,2048]{3,2,1,0:T(8,128)(2,1)} %broadcast_select_fusion), channel_id=1, replica_groups=mesh['dp'=2,'ep'=8] {'ep'}, dimensions={0} | all-to-all | bytes 134217728 | tf_op jit(solution)/shard_map/all_to_all | solution.py:69
  1326.3 44.1 %copy.37 = bf16[1,16,8,128,2048]{4,3,2,1,0:T(8,128)(2,1)} copy(bf16[1,16,8,128,2048]{4,3,1,2,0:T(8,128)(2,1)} %bitcast.18) | data formatting | bytes 134217728 | tf_op jit(solution)/shard_map/all_to_all | solution.py:69
  1370.4 77.4 %fusion.74 = f32[16,1024,768]{2,1,0:T(8,128)} fusion(bf16[16,1024,2048]{2,1,0:T(8,128)(2,1)} %bitcast.19, bf16[16,2048,768]{2,1,0:T(8,128)(2,1)} %param.19), kind=kOutput, calls=%fused_computation.105 | convolution fusion | flops 51539607552 | bytes 167772160 | tf_op jit(solution)/shard_map/ecd,edf->ecf/dot_general | solution.py:70
  1447.8 69.0 %multiply_convert_fusion.5 = bf16[16,1024,768]{2,1,0:T(8,128)(2,1)} fusion(f32[16,1024,768]{2,1,0:T(8,128)} %fusion.74, bf16[16,1024,2048]{2,1,0:T(8,128)(2,1)} %bitcast.19, bf16[16,2048,768]{2,1,0:T(8,128)(2,1)} %param.20), kind=kOutput, calls=%fused_computation.18.clone.clone.1 | convolution fusion | flops 51615105024 | bytes 192937984 | tf_op jit(solution)/shard_map/ecd,edf->ecf/dot_general | solution.py:71
  1516.8 64.6 %convert_bitcast_fusion = bf16[1,16,1024,2048]{3,2,1,0:T(8,128)(2,1)} fusion(bf16[16,768,2048]{2,1,0:T(8,128)(2,1)} %param.21, bf16[16,1024,768]{2,1,0:T(8,128)(2,1)} %multiply_convert_fusion.5), kind=kOutput, calls=%fused_computation.12 | convolution fusion | flops 51573161984 | bytes 142606336 | tf_op jit(solution)/shard_map/ecf,efd->ecd/dot_general | solution.py:73
  1581.4 57.2 %copy.38 = bf16[1,16,1024,2048]{3,1,0,2:T(8,128)(2,1)} copy(bf16[1,16,1024,2048]{3,2,1,0:T(8,128)(2,1)} %convert_bitcast_fusion) | data formatting | bytes 134217728 | tf_op jit(solution)/shard_map/reshape | solution.py:74
  1651.5 49.0 %gather_fusion = s32[8192]{0:T(1024)S(1)} fusion(s32[128]{0:T(128)S(1)} %copy-done.2, s32[8192]{0:T(1024)S(1)} %broadcast_clamp_fusion.3), kind=kCustom, calls=%fused_computation | custom fusion | bytes 98304 | tf_op jit(solution)/shard_map/jit(_take)/gather | solution.py:31
  1717.7 50.7 %gather_fusion.4 = f32[8192]{0:T(1024)S(1)} fusion(f32[1024,128]{1,0:T(8,128)S(1)} %fusion.23, s32[8192]{0:T(1024)S(1)} %reshape.451), kind=kCustom, calls=%fused_computation.4 | custom fusion | bytes 131072 | tf_op jit(solution)/shard_map/jit(take_along_axis)/gather | solution.py:65
  1778.0 632.2 %all-to-all-done.1 = bf16[1,16,1024,2048]{3,1,0,2:T(8,128)(2,1)} async-done(((bf16[1,16,1024,2048]{3,1,0,2:T(8,128)(2,1)}), bf16[1,16,1024,2048]{3,1,0,2:T(8,128)(2,1)}, u32[]{:S(2)}, u32[]{:S(2)}) %all-to-all-start.1) | async-done | bytes 67108896 | tf_op jit(solution)/shard_map/all_to_all | solution.py:74
  2410.3 57.7 %copy.39 = bf16[1,16,8,128,2048]{4,3,1,2,0:T(8,128)(2,1)} copy(bf16[1,16,8,128,2048]{4,1,3,2,0:T(8,128)(2,1)} %bitcast.21) | data formatting | bytes 134217728 | tf_op jit(solution)/shard_map/all_to_all | solution.py:74
  2468.0 190.9 %gather_fusion.3 = bf16[8192,2048]{1,0:T(8,128)(2,1)} fusion(bf16[16384,2048]{1,0:T(8,128)(2,1)} %bitcast.23, s32[8192]{0:T(1024)S(1)} %copy-done.12), kind=kCustom, calls=%fused_computation.3 | custom fusion | bytes 67141632 | tf_op jit(solution)/shard_map/jit(_take)/gather | solution.py:75
  2658.9 35.6 %multiply_reduce_fusion = f32[1024,2048]{1,0:T(8,128)} fusion(bf16[8192,2048]{1,0:T(8,128)(2,1)} %gather_fusion.3, f32[1024,8]{1,0:T(8,128)S(1)} %fusion.47, pred[1024,8]{1,0:T(8,128)(4,1)S(1)} %copy-done.8), kind=kLoop, calls=%fused_computation.11 | loop fusion | flops 65011712 | bytes 41984000 | tf_op jit(solution)/shard_map/reduce_sum | solution.py:76
  2694.5 16.1 fusion.42
  (99 shorter events, 61.2 us)
Async XLA Ops:
  6.5 1702.4 %copy-start = (f32[2048,128]{1,0:T(8,128)S(1)}, f32[2048,128]{1,0:T(8,128)}, u32[]{:S(2)}) copy-start(f32[2048,128]{1,0:T(8,128)} %param.18) | copy-start | bytes 3145732
  6.6 164.9 %all-gather.10.cloned.1.call-start = ((), (), s32[]{:S(2)}) async-start(), calls=%async_computation.3 | async-start | bytes 18874368 | tf_op jit(solution)/shard_map/all_gather | solution.py:51
  7.3 187.2 %all-gather.12.cloned.1.call-start = ((), (), s32[]{:S(2)}) async-start(), calls=%async_computation.4 | async-start | bytes 18874368 | tf_op jit(solution)/shard_map/all_gather | solution.py:52
  8.1 251.3 %all-gather.8.cloned.1.call-start = ((), (), s32[]{:S(2)}) async-start(), calls=%async_computation.2 | async-start | bytes 18874368 | tf_op jit(solution)/shard_map/all_gather | solution.py:53
  8.9 378.7 %all-gather.14.cloned.1.call-start = ((), (), s32[]{:S(2)}) async-start(), calls=%async_computation.5 | async-start | bytes 18874368 | tf_op jit(solution)/shard_map/all_gather | solution.py:54
  10.1 58.5 %copy-start.5 = (s32[1,1024,8]{2,1,0:T(8,128)}, s32[1,1024,8]{2,1,0:T(8,128)S(1)}, u32[]{:S(2)}) copy-start(s32[1,1024,8]{2,1,0:T(8,128)S(1)} %copy.34) | copy-start | bytes 98308
  10.6 158.9 %copy-start.9 = (s32[8192]{0:T(1024)}, s32[8192]{0:T(1024)S(1)}, u32[]{:S(2)}) copy-start(s32[8192]{0:T(1024)S(1)} %reshape_reshape.5) | copy-start | bytes 98308
  68.7 100.9 %copy-start.1 = (s32[128]{0:T(128)}, s32[128]{0:T(128)S(1)}, u32[]{:S(2)}) copy-start(s32[128]{0:T(128)S(1)} %sub.37) | copy-start | bytes 1540
  78.9 90.7 %copy-start.3 = (s32[8192]{0:T(1024)}, s32[8192]{0:T(1024)S(1)}, u32[]{:S(2)}) copy-start(s32[8192]{0:T(1024)S(1)} %get-tuple-element.7) | copy-start | bytes 98308
  411.4 4.7 copy-start.11
  416.2 124.1 %copy-start.16 = (pred[8,16,128]{2,1,0:T(8,128)(4,1)S(1)}, pred[8,16,128]{2,1,0:T(8,128)(4,1)}, u32[]{:S(2)}) copy-start(pred[8,16,128]{2,1,0:T(8,128)(4,1)} %compare_and_fusion) | copy-start | bytes 49156
  1638.6 12.3 copy-start.14
  1638.6 12.3 copy-start.15
  1638.7 771.6 %all-to-all-start.1 = ((bf16[1,16,1024,2048]{3,1,0,2:T(8,128)(2,1)}), bf16[1,16,1024,2048]{3,1,0,2:T(8,128)(2,1)}, u32[]{:S(2)}, u32[]{:S(2)}) async-start(bf16[1,16,1024,2048]{3,1,0,2:T(8,128)(2,1)} %copy.38), calls=%async_computation.1 | async-start | bytes 134217728 | tf_op jit(solution)/shard_map/all_to_all | solution.py:74
  1648.8 120.9 %all-gather.16.cloned.1.call-start = ((), (), s32[]{:S(2)}) async-start(), calls=%async_computation.6 | async-start | bytes 3538944 | tf_op jit(solution)/shard_map/all_gather | solution.py:77
  1649.5 1045.0 %all-gather.18.cloned.1.call-start = ((), (), s32[]{:S(2)}) async-start(), calls=%async_computation.7 | async-start | bytes 3538944 | tf_op jit(solution)/shard_map/all_gather | solution.py:78
  1650.1 1044.4 %all-gather.20.cloned.1.call-start = ((), (), s32[]{:S(2)}) async-start(), calls=%async_computation.8 | async-start | bytes 3538944 | tf_op jit(solution)/shard_map/all_gather | solution.py:79
  1651.4 49.1 %copy-start.4 = (s32[8192]{0:T(1024)S(1)}, s32[8192]{0:T(1024)}, u32[]{:S(2)}) copy-start(s32[8192]{0:T(1024)} %copy-done.3) | copy-start | bytes 98308
  1651.4 55.9 %copy-start.10 = (s32[8192]{0:T(1024)S(1)}, s32[8192]{0:T(1024)}, u32[]{:S(2)}) copy-start(s32[8192]{0:T(1024)} %copy-done.9) | copy-start | bytes 98308
  1651.4 57.5 %copy-start.18 = (f32[1024]{0:T(1024)S(1)}, f32[1024]{0:T(1024)}, u32[]{:S(2)}) copy-start(f32[1024]{0:T(1024)} %copy-done.17) | copy-start | bytes 12292
  1717.7 51.0 %copy-start.6 = (s32[1,1024,8]{2,1,0:T(8,128)S(1)}, s32[1,1024,8]{2,1,0:T(8,128)}, u32[]{:S(2)}) copy-start(s32[1,1024,8]{2,1,0:T(8,128)} %copy-done.5) | copy-start | bytes 98308
  1717.7 52.0 %copy-start.19 = (f32[1024]{0:T(1024)S(1)}, f32[1024]{0:T(1024)}, u32[]{:S(2)}) copy-start(f32[1024]{0:T(1024)} %copy-done.17) | copy-start | bytes 12292
  2410.3 57.7 %copy-start.12 = (s32[8192]{0:T(1024)S(1)}, s32[8192]{0:T(1024)}, u32[]{:S(2)}) copy-start(s32[8192]{0:T(1024)} %broadcast_clamp_fusion.2) | copy-start | bytes 98308
  2468.0 190.9 %copy-start.8 = (pred[1024,8]{1,0:T(8,128)(4,1)S(1)}, pred[1024,8]{1,0:T(8,128)(4,1)}, u32[]{:S(2)}) copy-start(pred[1024,8]{1,0:T(8,128)(4,1)} %broadcast_in_dim.73) | copy-start | bytes 24580
  (4 other events, 9.9 us)
Sparse Core Ops, SparseCore 0:
  9.0 83.9 all-gather.9
  94.5 81.6 all-gather.11
  177.8 81.6 all-gather.7
  260.9 81.6 all-gather.13
  1650.9 50.7 all-gather.15
  1703.1 49.3 all-gather.17
  1754.1 48.4 all-gather.19
where the time goes:
time: 2730 us; the launch traced here: 2720 us
  blocking collectives  742 us (27%)
  waiting for transfers between devices  679 us (25%)
  local copies, waits for them, and re-layouts  669 us (25%)
  matrix products  442 us (16%)
  other arithmetic  161 us (6%)
    all_to_all x1, blocking collectives, local_layer(): lax.all_to_all(send_buf, 'ep', 0, 2, tiled=True)  742 us
    all_to_all x1, waiting for transfers between devices, local_layer(): lax.all_to_all(expert_out.reshape(1, local_experts, group * capacity, d_m...  632 us
    gather x1, local copies, waits for them, and re-layouts, local_layer(): jnp.take(returned.reshape(n_experts * capacity, d_model), slot_of_assign,...  191 us
    gather x1, local copies, waits for them, and re-layouts, local_layer(): jnp.take(moe_in, slot_token, axis=0)  124 us
    gather x1, local copies, waits for them, and re-layouts, slot_plan(): slot_token = jnp.take(sort_order, slot_rows.reshape(-1)) // top_k  90.7 us
    dot_general x1, matrix products, local_layer(): jnp.einsum('ecd,edf->ecf', received, gate_loc, preferred_element_type=jnp...  77.4 us
    dot_general x1, matrix products, local_layer(): jnp.einsum('ecd,edf->ecf', received, up_loc, preferred_element_type=jnp.f...  69 us
    dot_general x1, matrix products, local_layer(): jnp.einsum('ecf,efd->ecd', middle, down_loc, preferred_element_type=jnp.f...  64.6 us
  transfers between devices with their start and end apart: 8, of which 2 were waited for; matrix products, arithmetic and copies ran while one was open for 27% of the time, Pallas kernels for 0%

commit v1 on v0

v1 whole, which is shorter than its diff:
```python
import functools
import jax
import jax.numpy as jnp
from jax import lax
from jax.experimental import pallas as pl
from jax.experimental.pallas import tpu as pltpu
from jax.sharding import PartitionSpec as P

EPSILON = 1e-6
HALVES = 2
PARTS = 2
CHUNKS = HALVES * PARTS
ROW_TILE = 192
LANES = 128
SUBLANES = 8
VMEM_BYTES = 66_000_000


def rms_norm(values):
    as_f32 = values.astype(jnp.float32)
    return as_f32 * lax.rsqrt(jnp.mean(as_f32 * as_f32, axis=-1, keepdims=True) + EPSILON)


def expert_kernel(count_ref, token_ref, gate_ref, u_hbm, gate_w, up_w, down_w, out_hbm, u_rows, acc, x_tiles, x_rows, middle, y_tiles, in_sem, out_sem):
    part, expert = pl.program_id(0), pl.program_id(1)
    n_local = pl.num_programs(1)
    group, unused, lane_blocks, unused = u_hbm.shape
    n_tok = u_rows.shape[0] - 1
    per_dev = n_tok // group
    dev_rows = per_dev * lane_blocks
    ff = gate_w.shape[2]
    d_model = gate_w.shape[1]
    row_tile = x_rows.shape[0]

    @pl.when(expert == 0)
    def _():
        loads = []
        for g in range(group):
            source = u_hbm.at[g, pl.ds(pl.multiple_of(part * per_dev, per_dev), per_dev)]
            loads.append(pltpu.make_async_copy(source, u_rows.at[pl.ds(g * per_dev, per_dev)], in_sem.at[g]))
            loads[-1].start()

        def clear(step, carry):
            acc[pl.ds(pl.multiple_of(step * 256, 256), 256), :] = jnp.zeros((256, LANES), jnp.float32)
            return carry

        lax.fori_loop(0, n_tok * lane_blocks // 256, clear, 0)
        for load in loads:
            load.wait()

    count = count_ref[part * n_local + expert]

    def one_tile(tile, carry):
        base = tile * row_tile
        live = jnp.minimum(count - base, row_tile)

        def gather(step, inner):
            for i in range(16):
                token = token_ref[0, 0, 0, base + step * 16 + i]
                group = step * 2 + i // SUBLANES
                start = group * (SUBLANES * lane_blocks) + i % SUBLANES
                x_tiles[pl.ds(start, lane_blocks, stride=SUBLANES), :] = u_rows[token].astype(jnp.float32)
            return inner

        steps = (live + 15) // 16
        lax.fori_loop(0, steps, gather, 0)

        def pack(step, inner):
            span = 2 * SUBLANES * lane_blocks
            tiles = x_tiles[pl.ds(pl.multiple_of(step * span, span), span), :].reshape(2, lane_blocks, SUBLANES, LANES)
            for c in range(lane_blocks):
                pair = jnp.concatenate([tiles[0, c], tiles[1, c]], axis=0).astype(jnp.bfloat16)
                x_rows[pl.ds(pl.multiple_of(step * 16, 16), 16), c * LANES:(c + 1) * LANES] = pair
            return inner

        lax.fori_loop(0, steps, pack, 0)

        for start in range(0, ff, 256):
            cols = slice(start, start + 256)
            gate_act = jnp.dot(x_rows[...], gate_w[0, :, cols], preferred_element_type=jnp.float32)
            up_act = jnp.dot(x_rows[...], up_w[0, :, cols], preferred_element_type=jnp.float32)
            middle[:, cols] = (jax.nn.silu(gate_act) * up_act).astype(jnp.bfloat16)
        for start in range(0, d_model, 256):
            rows_out = jnp.dot(middle[...], down_w[0, :, start:start + 256], preferred_element_type=jnp.float32)
            rows_out = rows_out.astype(jnp.bfloat16).astype(jnp.float32)
            for c in range(256 // LANES):
                for b in range(row_tile // SUBLANES):
                    at = (b * lane_blocks + start // LANES + c) * SUBLANES
                    y_tiles[at:at + SUBLANES, :] = rows_out[b * SUBLANES:(b + 1) * SUBLANES, c * LANES:(c + 1) * LANES]

        def combine(step, inner):
            places, sums = [], []
            for i in range(SUBLANES):
                token = token_ref[0, 0, 0, base + step * SUBLANES + i]
                weight = gate_ref[0, 0, 0, token]
                start = step * (SUBLANES * lane_blocks) + i
                row = y_tiles[pl.ds(start, lane_blocks, stride=SUBLANES), :]
                place = pl.ds(pl.multiple_of(token * lane_blocks, lane_blocks), lane_blocks)
                places.append(place)
                sums.append(acc[place, :] + weight * row)
            for place, total in zip(places, sums):
                acc[place, :] = total
            return inner

        lax.fori_loop(0, (live + SUBLANES - 1) // SUBLANES, combine, 0)
        return carry

    lax.fori_loop(0, (count + row_tile - 1) // row_tile, one_tile, 0)

    @pl.when(expert == n_local - 1)
    def _():
        stores = []
        for g in range(group):
            target = out_hbm.at[g, pl.ds(pl.multiple_of(part * dev_rows, dev_rows), dev_rows)]
            stores.append(pltpu.make_async_copy(acc.at[pl.ds(g * dev_rows, dev_rows)], target, out_sem.at[g]))
            stores[-1].start()
        for store in stores:
            store.wait()


def expert_partials(counts, token_lists, gate_table, u_all, gate_loc, up_loc, down_loc):
    group, held, lane_blocks, unused = u_all.shape
    n_local, d_model, ff = gate_loc.shape
    n_parts, unused, unused, list_len = token_lists.shape
    table_len = gate_table.shape[3]
    n_tok = group * held // n_parts
    rows = n_tok * lane_blocks
    grid_spec = pltpu.PrefetchScalarGridSpec(
        num_scalar_prefetch=1,
        grid=(n_parts, n_local),
        in_specs=[
            pl.BlockSpec((1, 1, 1, list_len), lambda p, e, c: (p, e, 0, 0), memory_space=pltpu.SMEM),
            pl.BlockSpec((1, 1, 1, table_len), lambda p, e, c: (p, e, 0, 0), memory_space=pltpu.SMEM),
            pl.BlockSpec(memory_space=pl.ANY),
            pl.BlockSpec((1, d_model, ff), lambda p, e, c: (e, 0, 0)),
            pl.BlockSpec((1, d_model, ff), lambda p, e, c: (e, 0, 0)),
            pl.BlockSpec((1, ff, d_model), lambda p, e, c: (e, 0, 0)),
        ],
        out_specs=pl.BlockSpec(memory_space=pl.ANY),
        scratch_shapes=[
            pltpu.VMEM((n_tok + 1, lane_blocks, LANES), jnp.bfloat16),
            pltpu.VMEM((rows + lane_blocks, LANES), jnp.float32),
            pltpu.VMEM((ROW_TILE * lane_blocks, LANES), jnp.float32),
            pltpu.VMEM((ROW_TILE, d_model), jnp.bfloat16),
            pltpu.VMEM((ROW_TILE, ff), jnp.bfloat16),
            pltpu.VMEM((ROW_TILE * lane_blocks, LANES), jnp.float32),
            pltpu.SemaphoreType.DMA((group,)),
            pltpu.SemaphoreType.DMA((group,)),
        ],
    )
    flops = 6 * n_parts * n_tok * d_model * ff
    return pl.pallas_call(
        expert_kernel,
        grid_spec=grid_spec,
        out_shape=jax.ShapeDtypeStruct((group, held * lane_blocks, LANES), jnp.float32),
        compiler_params=pltpu.CompilerParams(dimension_semantics=('arbitrary', 'arbitrary'), vmem_limit_bytes=VMEM_BYTES),
        cost_estimate=pl.CostEstimate(flops=flops, bytes_accessed=n_parts * (3 * n_local * d_model * ff * 2 + rows * LANES * 6), transcendentals=0),
        name='routed_experts',
    )(counts, token_lists, gate_table, u_all, gate_loc, up_loc, down_loc)


def local_layer(x_loc, q_shard, k_shard, v_shard, o_shard, w_router, gate_loc, up_loc, down_loc, sgate_shard, sup_shard, sdown_shard, ids_loc, group):
    n_seq, seq_len, d_model = x_loc.shape
    n_heads, head_dim = q_shard.shape[1:]
    n_tok = n_seq * seq_len
    top_k = ids_loc.shape[-1]
    n_local = gate_loc.shape[0]
    n_experts = n_local * group
    lane_blocks = d_model // LANES
    per_chunk = n_tok // CHUNKS
    chunk_tok = group * per_chunk
    per_half = n_tok // HALVES
    first_expert = lax.axis_index('ep') * n_local

    query_w = lax.all_gather(q_shard, 'ep', axis=0, tiled=True)
    key_w = lax.all_gather(k_shard, 'ep', axis=0, tiled=True)
    value_w = lax.all_gather(v_shard, 'ep', axis=0, tiled=True)
    out_w = lax.all_gather(o_shard, 'ep', axis=0, tiled=True)

    ids_t = ids_loc.reshape(n_tok, top_k).T
    ids_all = lax.all_gather(ids_t, 'ep', axis=0)
    local_ids = jnp.arange(n_local, dtype=jnp.int32)[:, None, None, None] + first_expert
    chosen = ids_all[None] == local_ids
    member = jnp.any(chosen, axis=2).reshape(n_local, group, CHUNKS, per_chunk).transpose(2, 0, 1, 3).reshape(CHUNKS, n_local, chunk_tok)
    counts = jnp.sum(member.astype(jnp.int32), axis=-1)
    token_lists = lax.sort(jnp.where(member, jnp.arange(chunk_tok, dtype=jnp.int32), chunk_tok), dimension=2, is_stable=False)

    normed = rms_norm(x_loc).astype(jnp.bfloat16)
    queries = jnp.einsum('bsd,dhe->bshe', normed, query_w, preferred_element_type=jnp.float32).astype(jnp.bfloat16)
    normed_k, token_lists, counts = lax.optimization_barrier((normed, token_lists, counts))
    keys_all = jnp.einsum('bsd,dhe->bshe', normed_k, key_w, preferred_element_type=jnp.float32).astype(jnp.bfloat16)
    scores = jnp.einsum('bqhe,bkhe->bhqk', queries, keys_all, preferred_element_type=jnp.float32) * (head_dim ** -0.5)
    causal = jnp.arange(seq_len)[:, None] >= jnp.arange(seq_len)[None, :]
    attn_probs = jax.nn.softmax(jnp.where(causal, scores, -1e30), axis=-1).astype(jnp.bfloat16)
    normed_v, attn_probs = lax.optimization_barrier((normed, attn_probs))
    vals_all = jnp.einsum('bsd,dhe->bshe', normed_v, value_w, preferred_element_type=jnp.float32).astype(jnp.bfloat16)
    attended = jnp.einsum('bhqk,bkhe->bqhe', attn_probs, vals_all, preferred_element_type=jnp.float32).astype(jnp.bfloat16)
    attended = attended.reshape(n_tok, n_heads * head_dim)
    x_flat = x_loc.reshape(n_tok, d_model)

    residuals, inputs, u_alls, gates = [], [], [], []
    tok_ids = ids_loc.reshape(n_tok, top_k)
    for half in range(HALVES):
        rows = slice(half * per_half, (half + 1) * per_half)
        attn_out = jnp.dot(attended[rows], out_w, preferred_element_type=jnp.float32).astype(jnp.bfloat16)
        residual = (x_flat[rows].astype(jnp.float32) + attn_out.astype(jnp.float32)).astype(jnp.bfloat16)
        residual = lax.optimization_barrier(residual)
        hidden = rms_norm(residual)
        moe_in = hidden.astype(jnp.bfloat16)
        sent, attended = lax.optimization_barrier((moe_in.reshape(per_half, lane_blocks, LANES), attended))
        u_alls.append(lax.all_gather(sent, 'ep', axis=0))
        logits = jnp.dot(hidden, w_router, precision=lax.Precision.HIGHEST, preferred_element_type=jnp.float32)
        hit = tok_ids[rows][:, :, None] == jnp.arange(n_experts, dtype=jnp.int32)
        picked = jnp.sum(jnp.where(hit, logits[:, None, :], 0.0), axis=-1)
        gates.append(jax.nn.softmax(picked, axis=-1))
        residuals.append(residual)
        inputs.append(moe_in)

    gates_t = jnp.concatenate(gates, axis=0).T
    gates_all = lax.all_gather(gates_t, 'ep', axis=0)
    gate_table = jnp.sum(jnp.where(chosen, gates_all[None], 0.0), axis=2)
    gate_table = gate_table.reshape(n_local, group, CHUNKS, per_chunk).transpose(2, 0, 1, 3).reshape(CHUNKS, n_local, 1, chunk_tok)
    gate_table = jnp.pad(gate_table, ((0, 0), (0, 0), (0, 0), (0, LANES)))

    ff_rows, ff_shared = sgate_shard.shape
    shards = jnp.concatenate([sgate_shard, sup_shard, sdown_shard.reshape(-1, ff_shared)], axis=0)
    shards, moe_in = lax.optimization_barrier((shards, jnp.concatenate(inputs, axis=0)))
    shared_all = lax.all_gather(shards, 'ep', axis=0)
    shared_gate = shared_all[:, :ff_rows].reshape(-1, ff_shared)
    shared_up = shared_all[:, ff_rows:2 * ff_rows].reshape(-1, ff_shared)
    shared_down = shared_all[:, 2 * ff_rows:].reshape(-1, d_model)

    gate_act = jnp.dot(moe_in, shared_gate, preferred_element_type=jnp.float32)
    up_act = jnp.dot(moe_in, shared_up, preferred_element_type=jnp.float32)
    shared = jnp.dot((jax.nn.silu(gate_act) * up_act).astype(jnp.bfloat16), shared_down, preferred_element_type=jnp.float32).astype(jnp.bfloat16)

    outs = []
    for half in range(HALVES):
        parts = slice(half * PARTS, (half + 1) * PARTS)
        rows = slice(half * per_half, (half + 1) * per_half)
        partial = expert_partials(counts[parts].reshape(-1), token_lists[parts][:, :, None, :], gate_table[parts], u_alls[half], gate_loc, up_loc, down_loc)
        routed = lax.psum_scatter(partial.reshape(-1, LANES), 'ep', scatter_dimension=0, tiled=True).reshape(per_half, d_model)
        outs.append((residuals[half].astype(jnp.float32) + routed + shared[rows].astype(jnp.float32)).astype(jnp.bfloat16))
    return jnp.concatenate(outs, axis=0).reshape(n_seq, seq_len, d_model)


def solution(mesh):
    tok_spec = P(('dp', 'ep'), None, None)
    row_spec = P('ep', None)
    cube_spec = P('ep', None, None)
    in_specs = (tok_spec, cube_spec, cube_spec, cube_spec, row_spec, P(None, None), cube_spec, cube_spec, cube_spec, row_spec, row_spec, row_spec, tok_spec)
    return jax.shard_map(functools.partial(local_layer, group=mesh.shape['ep']), mesh=mesh, in_specs=in_specs, out_specs=tok_spec, check_vma=False)
```

time: 2730 us -> 964 us (0.35)
  blocking collectives: 742 us -> 48.1 us
  local copies, waits for them, and re-layouts: 669 us -> 40.8 us
  waiting for transfers between devices: 679 us -> 246 us
  Pallas kernels: 0 us -> 265 us
  matrix products: 442 us -> 228 us
  other arithmetic: 161 us -> 117 us
    all_to_all x1 -> x0, blocking collectives: 742 us -> none  [local_layer(): lax.all_to_all(send_buf, 'ep', 0, 2, tiled=True)]
    all_to_all x1 -> x0, waiting for transfers between devices: 632 us -> none  [local_layer(): lax.all_to_all(expert_out.reshape(1, local_experts, group * capacity, d_m...]
    gather x8 -> x0, local copies, waits for them, and re-layouts: 506 us -> none  [the longest x1 191 us: local_layer(): jnp.take(returned.reshape(n_experts * capacity, d_model), slot_of_assign,...]
    pallas_call x0 -> x2, Pallas kernels: none -> 265 us  [expert_partials(): pl.pallas_call(expert_kernel, grid_spec=grid_spec, out_shape=jax.ShapeDty...]
    dot_general x10 -> x8, matrix products: 376 us -> 147 us  [the longest x1 29.3 us: local_layer(): jnp.einsum('bhqk,bkhe->bqhe', attn_probs, vals_all, preferred_element_typ...]
    reduce_scatter x0 -> x2, waiting for transfers between devices: none -> 169 us  [local_layer(): lax.psum_scatter(partial.reshape(-1, LANES), 'ep', scatter_dimension=0, t...]
    all_to_all x2 -> x0, local copies, waits for them, and re-layouts: 102 us -> none  [the longest x1 57.7 us: local_layer(): lax.all_to_all(expert_out.reshape(1, local_experts, group * capacity, d_m...]
    div x0 -> x1, matrix products: none -> 73 us  [local_layer(): jax.nn.softmax(jnp.where(causal, scores, -1e+30), axis=-1)]
  transfers between devices with their start and end apart: 8 -> 9, of which waited for: 2 -> 5; matrix products, arithmetic and copies ran while one was open for 27% -> 35% of each run, Pallas kernels for 0% -> 28%
where the time goes in v1:
time: 964 us; the launch traced here: 960 us
  Pallas kernels  265 us (27%)
  waiting for transfers between devices  246 us (26%)
  matrix products  228 us (24%)
  other arithmetic  117 us (12%)
  blocking collectives  48.1 us (5%)
  local copies, waits for them, and re-layouts  40.8 us (4%)
  between operations  13.8 us (1%)
    pallas_call x2, Pallas kernels, expert_partials(): pl.pallas_call(expert_kernel, grid_spec=grid_spec, out_shape=jax.ShapeDty...  265 us
    reduce_scatter x2, waiting for transfers between devices, local_layer(): lax.psum_scatter(partial.reshape(-1, LANES), 'ep', scatter_dimension=0, t...  169 us
    div x1, matrix products, local_layer(): jax.nn.softmax(jnp.where(causal, scores, -1e+30), axis=-1)  73 us
    sort x1, other arithmetic, local_layer(): lax.sort(jnp.where(member, jnp.arange(chunk_tok, dtype=jnp.int32), chunk_...  72.4 us
    all_gather x1, waiting for transfers between devices, local_layer(): key_w = lax.all_gather(k_shard, 'ep', axis=0, tiled=True)  41.7 us
    dot_general x1, matrix products, local_layer(): jnp.einsum('bhqk,bkhe->bqhe', attn_probs, vals_all, preferred_element_typ...  29.3 us
    dot_general x2, matrix products, local_layer(): jnp.dot(attended[rows], out_w, preferred_element_type=jnp.float32)  27.9 us
    all_gather x1, blocking collectives, local_layer(): ids_all = lax.all_gather(ids_t, 'ep', axis=0)  25.3 us
  transfers between devices with their start and end apart: 9, of which 5 were waited for; matrix products, arithmetic and copies ran while one was open for 35% of the time, Pallas kernels for 28%

profile of v1, /device:TPU:112, one launch (start us, length us, event | category | flops | bytes accessed | tf_op | source)
XLA Modules:
  0.0 959.6 jit_solution(14114303616228290907)
XLA Ops:
  9.6 25.3 %all-gather = s32[64,1024]{1,0:T(8,128)S(1)} all-gather(s32[8,1024]{1,0:T(8,128)S(1)} %bitcast.105), channel_id=2, replica_groups=mesh['dp'=2,'ep'=8] {'ep'}, dimensions={0}, use_global_device_ids=true | all-gather | bytes 294912 | tf_op jit(solution)/shard_map/all_gather | solution.py:181
  37.7 72.4 %sort.7 = s32[4,16,2048]{2,0,1:T(4,128)} sort(s32[4,16,2048]{2,0,1:T(4,128)S(1)} %iota_select_fusion), dimensions={2}, to_apply=%region_2.3 | sort | flops 2228224 | bytes 1048576 | tf_op jit(solution)/shard_map/sort | solution.py:186
  118.1 23.1 %fusion.24 = bf16[1024,32,128]{2,0,1:T(8,128)(2,1)} fusion(bf16[2048,32,128]{2,1,0:T(8,128)(2,1)} %all-gather.13.cloned.1.call-done, bf16[1,1024,2048]{2,1,0:T(8,128)(2,1)} %fusion.18), kind=kOutput, calls=%fused_computation.24 | convolution fusion | flops 17184063488 | bytes 29360128 | tf_op jit(solution)/shard_map/bsd,dhe->bshe/dot_general | solution.py:189
  141.2 41.7 %all-gather.15.cloned.1.call-done = bf16[2048,32,128]{2,1,0:T(8,128)(2,1)} async-done(((bf16[256,32,128]{2,1,0:T(8,128)(2,1)}), bf16[2048,32,128]{2,1,0:T(8,128)(2,1)}) %all-gather.15.cloned.1.call-update) | async-done | bytes 16777232 | tf_op jit(solution)/shard_map/all_gather | solution.py:176
  182.9 23.0 %fusion.27 = bf16[1024,32,128]{2,0,1:T(8,128)(2,1)} fusion(bf16[2048,32,128]{2,1,0:T(8,128)(2,1)} %all-gather.15.cloned.1.call-done, bf16[1,1024,2048]{2,1,0:T(8,128)(2,1)} %fusion.18), kind=kOutput, calls=%fused_computation.25 | convolution fusion | flops 17184063488 | bytes 29360128 | tf_op jit(solution)/shard_map/bsd,dhe->bshe/dot_general | solution.py:191
  205.8 73.0 %fusion.7 = bf16[1,32,1024,1024]{2,3,1,0:T(8,128)(2,1)} fusion(pred[1024,1024]{0,1:T(8,128)(4,1)S(1)} %iota_compare_fusion, bf16[1024,32,128]{2,0,1:T(8,128)(2,1)} %fusion.24, bf16[1024,32,128]{2,0,1:T(8,128)(2,1)} %fusion.27), kind=kOutput, calls=%fused_computation.10 | convolution fusion | flops 8757774336 | bytes 84934656 | tf_op jit(solution)/shard_map/div | solution.py:194
  278.8 23.0 %fusion.101 = bf16[1024,32,128]{2,0,1:T(8,128)(2,1)} fusion(bf16[2048,32,128]{2,1,0:T(8,128)(2,1)} %all-gather.17.cloned.1.call-done, bf16[1,1024,2048]{2,1,0:T(8,128)(2,1)} %fusion.18), kind=kOutput, calls=%fused_computation.23.clone.clone.clone.1 | convolution fusion | flops 17184063488 | bytes 29360128 | tf_op jit(solution)/shard_map/bsd,dhe->bshe/dot_general | solution.py:196
  301.8 29.3 %fusion.30 = bf16[32,128,1024]{2,1,0:T(8,128)(2,1)} fusion(bf16[1,32,1024,1024]{2,3,1,0:T(8,128)(2,1)} %fusion.7, bf16[1024,32,128]{2,0,1:T(8,128)(2,1)} %fusion.101), kind=kOutput, calls=%fused_computation.26 | convolution fusion | flops 8594128896 | bytes 83886080 | tf_op jit(solution)/shard_map/bhqk,bkhe->bqhe/dot_general | solution.py:197
  335.7 13.5 %all-gather.19.cloned.1.call-done = bf16[4096,2048]{1,0:T(8,128)(2,1)} async-done(((bf16[512,2048]{1,0:T(8,128)(2,1)}), bf16[4096,2048]{1,0:T(8,128)(2,1)}) %all-gather.19.cloned.1.call-update) | async-done | bytes 16777232 | tf_op jit(solution)/shard_map/all_gather | solution.py:178
  349.3 13.9 %fusion.49 = bf16[512,2048]{1,0:T(8,128)(2,1)S(1)} fusion(bf16[512,4096]{0,1:T(8,128)(2,1)} %bitcast.96, bf16[4096,2048]{1,0:T(8,128)(2,1)} %all-gather.19.cloned.1.call-done, bf16[1,1024,2048]{2,1,0:T(8,128)(2,1)} %param.13), kind=kOutput, calls=%fused_computation.51 | convolution fusion | flops 8595177472 | bytes 25165824 | tf_op jit(solution)/shard_map/dot_general | solution.py:205
  366.1 13.9 %fusion.48 = bf16[512,2048]{1,0:T(8,128)(2,1)S(1)} fusion(bf16[4096,2048]{1,0:T(8,128)(2,1)} %all-gather.19.cloned.1.call-done, bf16[1024,4096]{0,1:T(8,128)(2,1)} %bitcast.90, bf16[1,1024,2048]{2,1,0:T(8,128)(2,1)} %param.13), kind=kOutput, calls=%fused_computation.49 | convolution fusion | flops 8595177472 | bytes 25165824 | tf_op jit(solution)/shard_map/dot_general | solution.py:205
  397.4 5.1 fusion.40
  402.5 8.2 select_reduce_fusion
  414.5 8.2 select_reduce_fusion.1
  423.0 22.8 %all-gather.1 = f32[64,1024]{1,0:T(8,128)S(1)} all-gather(f32[8,1024]{1,0:T(8,128)S(1)} %maximum_bitcast_fusion.1), channel_id=3, replica_groups=mesh['dp'=2,'ep'=8] {'ep'}, dimensions={0}, use_global_device_ids=true | all-gather | bytes 294912 | tf_op jit(solution)/shard_map/all_gather | solution.py:220
  449.1 17.4 %all-gather.25.cloned.1.call-done = bf16[4096,16,128]{2,1,0:T(8,128)(2,1)} async-done(((bf16[512,16,128]{2,1,0:T(8,128)(2,1)}), bf16[4096,16,128]{2,1,0:T(8,128)(2,1)}) %all-gather.25.cloned.1.call-update) | async-done | bytes 16777232 | tf_op jit(solution)/shard_map/all_gather | solution.py:211
  466.4 132.3 %routed_experts.3 = f32[8,8192,128]{2,1,0:T(8,128)} custom-call(s32[32]{0:T(128)} %reshape.175.count_ref, s32[2,16,1,2048]{3,2,1,0:T(1,128)} %broadcast_in_dim.82.token_ref, f32[2,16,1,2176]{3,2,1,0:T(1,128)} %get-tuple-element.31.gate_ref, bf16[8,512,16,128]{3,2,1,0:T(8,128)(2,1)} %bitcast.92, bf16[16,2048,768]{2,1,0:T(8,128)(2,1)} %gate_w.3, ...), custom_call_target="tpu_custom_call" | custom-call | flops 38654705664 | bytes 352321536 | tf_op jit(solution)/shard_map/routed_experts/pallas_call | solution.py:152
  601.3 132.4 %routed_experts.2 = f32[8,8192,128]{2,1,0:T(8,128)} custom-call(s32[32]{0:T(128)} %reshape.164.count_ref, s32[2,16,1,2048]{3,2,1,0:T(1,128)} %broadcast_in_dim.76.token_ref, f32[2,16,1,2176]{3,2,1,0:T(1,128)} %get-tuple-element.30.gate_ref, bf16[8,512,16,128]{3,2,1,0:T(8,128)(2,1)} %bitcast.91, bf16[16,2048,768]{2,1,0:T(8,128)(2,1)} %gate_w.3, ...), custom_call_target="tpu_custom_call" | custom-call | flops 38654705664 | bytes 352321536 | tf_op jit(solution)/shard_map/routed_experts/pallas_call | solution.py:152
  733.9 5.8 fusion.70
  744.2 8.3 fusion.75
  752.5 12.2 %convolution_convert_fusion = bf16[1024,2048]{1,0:T(8,128)(2,1)} fusion(bf16[768,2048]{1,0:T(8,128)(2,1)} %reshape.174, f32[1024,768]{1,0:T(8,128)} %fusion.75, bf16[1024,2048]{1,0:T(8,128)(2,1)} %pad_maximum_fusion, bf16[2048,768]{1,0:T(8,128)(2,1)S(1)} %bitcast.97), kind=kOutput, calls=%fused_computation.58 | convolution fusion | flops 6449266688 | bytes 17825792 | tf_op jit(solution)/shard_map/dot_general | solution.py:235
  764.8 5.9 reduce-scatter.5.cloned.1.call-done
  775.5 163.6 %reduce-scatter.3.cloned.1.call-done = f32[8192,128]{1,0:T(8,128)} async-done(((f32[65536,128]{1,0:T(8,128)}), f32[8192,128]{1,0:T(8,128)}) %reduce-scatter.3.cloned.1.call-update) | async-done | bytes 4194320 | tf_op jit(solution)/shard_map/reduce_scatter | solution.py:242
  944.0 6.3 fusion.44
  (107 shorter events, 65.3 us)
Async XLA Ops:
  6.5 3.1 copy-start.11
  6.5 111.5 %all-gather.13.cloned.1.call-start = ((), (), s32[]{:S(2)}) async-start(), calls=%async_computation.2 | async-start | bytes 18874368 | tf_op jit(solution)/shard_map/all_gather | solution.py:175
  7.3 175.5 %all-gather.15.cloned.1.call-start = ((), (), s32[]{:S(2)}) async-start(), calls=%async_computation.3 | async-start | bytes 18874368 | tf_op jit(solution)/shard_map/all_gather | solution.py:176
  8.1 270.7 %all-gather.17.cloned.1.call-start = ((), (), s32[]{:S(2)}) async-start(), calls=%async_computation.4 | async-start | bytes 18874368 | tf_op jit(solution)/shard_map/all_gather | solution.py:177
  8.9 340.3 %all-gather.19.cloned.1.call-start = ((), (), s32[]{:S(2)}) async-start(), calls=%async_computation.5 | async-start | bytes 18874368 | tf_op jit(solution)/shard_map/all_gather | solution.py:178
  9.6 456.9 %all-gather.25.cloned.1.call-start = ((), (), s32[]{:S(2)}) async-start(), calls=%async_computation.10 | async-start | bytes 18874368 | tf_op jit(solution)/shard_map/all_gather | solution.py:211
  34.9 2.4 copy-start.14
  110.1 4.9 copy-start.3
  363.2 47.8 %copy-start = (bf16[512,2048]{1,0:T(8,128)(2,1)}, bf16[512,2048]{1,0:T(8,128)(2,1)S(1)}, u32[]{:S(2)}) copy-start(bf16[512,2048]{1,0:T(8,128)(2,1)S(1)} %fusion.49) | copy-start | bytes 6291460
  380.1 2.9 copy-start.2
  381.1 4.6 copy-start.9
  381.1 4.6 copy-start.10
  383.1 218.3 %all-gather.21.cloned.1.call-start = ((), (), s32[]{:S(2)}) async-start(), calls=%async_computation.8 | async-start | bytes 18874368 | tf_op jit(solution)/shard_map/all_gather | solution.py:211
  383.7 350.2 %all-gather.23.cloned.1.call-start = ((), (), s32[]{:S(2)}) async-start(), calls=%async_computation.9 | async-start | bytes 10616832 | tf_op jit(solution)/shard_map/all_gather | solution.py:228
  389.2 2.8 copy-start.12
  391.8 4.8 copy-start.13
  391.8 5.6 copy-start.4
  391.9 378.7 %reduce-scatter.5.cloned.1.call-start = ((), (), s32[]{:S(2)}) async-start(), calls=%async_computation.7 | async-start | bytes 37748736 | tf_op jit(solution)/shard_map/reduce_scatter | solution.py:242
  397.4 48.4 %copy-start.15 = (s32[16]{0:T(128)S(1)}, s32[16]{0:T(128)}, u32[]{:S(2)}) copy-start(s32[16]{0:T(128)} %copy-done.14) | copy-start | bytes 196
  411.0 34.9 %copy-start.7 = (s32[64,1024]{1,0:T(8,128)S(1)}, s32[64,1024]{1,0:T(8,128)}, u32[]{:S(2)}) copy-start(s32[64,1024]{1,0:T(8,128)} %copy-done.6) | copy-start | bytes 786436
  598.8 1.0 copy-start.8
  598.8 340.3 %reduce-scatter.3.cloned.1.call-start = ((), (), s32[]{:S(2)}) async-start(), calls=%async_computation.6 | async-start | bytes 37748736 | tf_op jit(solution)/shard_map/reduce_scatter | solution.py:242
  744.2 8.3 copy-start.5
  775.5 168.5 %copy-start.1 = (bf16[512,2048]{1,0:T(8,128)(2,1)S(1)}, bf16[512,2048]{1,0:T(8,128)(2,1)}, u32[]{:S(2)}) copy-start(bf16[512,2048]{1,0:T(8,128)(2,1)} %copy-done) | copy-start | bytes 6291460
  (1 other events, 0.7 us)
Sparse Core Ops, SparseCore 0:
  9.0 89.1 all-gather.12
  99.7 83.0 all-gather.14
  184.5 81.6 all-gather.16
  267.6 81.6 all-gather.18
  383.2 83.1 all-gather.24
  467.9 81.6 all-gather.20
  551.1 50.4 all-gather.22
  603.9 166.6 reduce-scatter.4
  773.0 166.0 reduce-scatter.2

commit v2 on v1

--- a/solution.py
+++ b/solution.py
@@ -21,7 +21,7 @@
     return as_f32 * lax.rsqrt(jnp.mean(as_f32 * as_f32, axis=-1, keepdims=True) + EPSILON)
 
 
-def expert_kernel(count_ref, token_ref, gate_ref, u_hbm, gate_w, up_w, down_w, out_hbm, u_rows, acc, x_tiles, x_rows, middle, y_tiles, in_sem, out_sem):
+def expert_kernel(first_part, count_ref, token_ref, gate_ref, u_hbm, gate_w, up_w, down_w, out_hbm, u_rows, acc, x_tiles, x_rows, middle, y_tiles, in_sem, out_sem):
     part, expert = pl.program_id(0), pl.program_id(1)
     n_local = pl.num_programs(1)
     group, unused, lane_blocks, unused = u_hbm.shape
@@ -36,7 +36,7 @@
     def _():
         loads = []
         for g in range(group):
-            source = u_hbm.at[g, pl.ds(pl.multiple_of(part * per_dev, per_dev), per_dev)]
+            source = u_hbm.at[g, pl.ds(pl.multiple_of((first_part + part) * per_dev, per_dev), per_dev)]
             loads.append(pltpu.make_async_copy(source, u_rows.at[pl.ds(g * per_dev, per_dev)], in_sem.at[g]))
             loads[-1].start()
 
@@ -118,12 +118,12 @@
             store.wait()
 
 
-def expert_partials(counts, token_lists, gate_table, u_all, gate_loc, up_loc, down_loc):
+def expert_partials(counts, token_lists, gate_table, u_all, gate_loc, up_loc, down_loc, first_part):
     group, held, lane_blocks, unused = u_all.shape
     n_local, d_model, ff = gate_loc.shape
     n_parts, unused, unused, list_len = token_lists.shape
     table_len = gate_table.shape[3]
-    n_tok = group * held // n_parts
+    n_tok = list_len
     rows = n_tok * lane_blocks
     grid_spec = pltpu.PrefetchScalarGridSpec(
         num_scalar_prefetch=1,
@@ -150,9 +150,9 @@
     )
     flops = 6 * n_parts * n_tok * d_model * ff
     return pl.pallas_call(
-        expert_kernel,
+        functools.partial(expert_kernel, first_part),
         grid_spec=grid_spec,
-        out_shape=jax.ShapeDtypeStruct((group, held * lane_blocks, LANES), jnp.float32),
+        out_shape=jax.ShapeDtypeStruct((group, n_parts * rows // group, LANES), jnp.float32),
         compiler_params=pltpu.CompilerParams(dimension_semantics=('arbitrary', 'arbitrary'), vmem_limit_bytes=VMEM_BYTES),
         cost_estimate=pl.CostEstimate(flops=flops, bytes_accessed=n_parts * (3 * n_local * d_model * ff * 2 + rows * LANES * 6), transcendentals=0),
         name='routed_experts',
@@ -194,6 +194,10 @@
     attn_probs = jax.nn.softmax(jnp.where(causal, scores, -1e30), axis=-1).astype(jnp.bfloat16)
     normed_v, attn_probs = lax.optimization_barrier((normed, attn_probs))
     vals_all = jnp.einsum('bsd,dhe->bshe', normed_v, value_w, preferred_element_type=jnp.float32).astype(jnp.bfloat16)
+    ff_rows, ff_shared = sgate_shard.shape
+    shards = jnp.concatenate([sgate_shard, sup_shard, sdown_shard.reshape(-1, ff_shared)], axis=0)
+    shards, vals_all = lax.optimization_barrier((shards, vals_all))
+    shared_all = lax.all_gather(shards, 'ep', axis=0)
     attended = jnp.einsum('bhqk,bkhe->bqhe', attn_probs, vals_all, preferred_element_type=jnp.float32).astype(jnp.bfloat16)
     attended = attended.reshape(n_tok, n_heads * head_dim)
     x_flat = x_loc.reshape(n_tok, d_model)
@@ -208,6 +212,8 @@
         hidden = rms_norm(residual)
         moe_in = hidden.astype(jnp.bfloat16)
         sent, attended = lax.optimization_barrier((moe_in.reshape(per_half, lane_blocks, LANES), attended))
+        if half == 0:
+            sent, shared_all = lax.optimization_barrier((sent, shared_all))
         u_alls.append(lax.all_gather(sent, 'ep', axis=0))
         logits = jnp.dot(hidden, w_router, precision=lax.Precision.HIGHEST, preferred_element_type=jnp.float32)
         hit = tok_ids[rows][:, :, None] == jnp.arange(n_experts, dtype=jnp.int32)
@@ -222,10 +228,7 @@
     gate_table = gate_table.reshape(n_local, group, CHUNKS, per_chunk).transpose(2, 0, 1, 3).reshape(CHUNKS, n_local, 1, chunk_tok)
     gate_table = jnp.pad(gate_table, ((0, 0), (0, 0), (0, 0), (0, LANES)))
 
-    ff_rows, ff_shared = sgate_shard.shape
-    shards = jnp.concatenate([sgate_shard, sup_shard, sdown_shard.reshape(-1, ff_shared)], axis=0)
-    shards, moe_in = lax.optimization_barrier((shards, jnp.concatenate(inputs, axis=0)))
-    shared_all = lax.all_gather(shards, 'ep', axis=0)
+    moe_in = jnp.concatenate(inputs, axis=0)
     shared_gate = shared_all[:, :ff_rows].reshape(-1, ff_shared)
     shared_up = shared_all[:, ff_rows:2 * ff_rows].reshape(-1, ff_shared)
     shared_down = shared_all[:, 2 * ff_rows:].reshape(-1, d_model)
@@ -235,12 +238,14 @@
     shared = jnp.dot((jax.nn.silu(gate_act) * up_act).astype(jnp.bfloat16), shared_down, preferred_element_type=jnp.float32).astype(jnp.bfloat16)
 
     outs = []
-    for half in range(HALVES):
-        parts = slice(half * PARTS, (half + 1) * PARTS)
-        rows = slice(half * per_half, (half + 1) * per_half)
-        partial = expert_partials(counts[parts].reshape(-1), token_lists[parts][:, :, None, :], gate_table[parts], u_alls[half], gate_loc, up_loc, down_loc)
-        routed = lax.psum_scatter(partial.reshape(-1, LANES), 'ep', scatter_dimension=0, tiled=True).reshape(per_half, d_model)
-        outs.append((residuals[half].astype(jnp.float32) + routed + shared[rows].astype(jnp.float32)).astype(jnp.bfloat16))
+    for first, count in ((0, 1), (1, 1), (2, 2)):
+        parts = slice(first, first + count)
+        half, first_part = first // PARTS, first % PARTS
+        in_half = slice(first_part * per_chunk, (first_part + count) * per_chunk)
+        rows = slice(first * per_chunk, (first + count) * per_chunk)
+        partial = expert_partials(counts[parts].reshape(-1), token_lists[parts][:, :, None, :], gate_table[parts], u_alls[half], gate_loc, up_loc, down_loc, first_part)
+        routed = lax.psum_scatter(partial.reshape(-1, LANES), 'ep', scatter_dimension=0, tiled=True).reshape(count * per_chunk, d_model)
+        outs.append((residuals[half][in_half].astype(jnp.float32) + routed + shared[rows].astype(jnp.float32)).astype(jnp.bfloat16))
     return jnp.concatenate(outs, axis=0).reshape(n_seq, seq_len, d_model)
 
 

time: 964 us -> 959 us (level)
  waiting for transfers between devices: 246 us -> 218 us
    reduce_scatter x2 -> x3, waiting for transfers between devices: 169 us -> 116 us  [local_layer(): lax.psum_scatter(partial.reshape(-1, LANES), 'ep', scatter_dimension=0, t...]
    all_gather x1, waiting for transfers between devices: 0.02 us -> 35 us  [local_layer(): shared_all = lax.all_gather(shards, 'ep', axis=0)]
    pallas_call x2 -> x3, Pallas kernels: 265 us -> 268 us  [expert_partials(): pl.pallas_call(functools.partial(expert_kernel, first_part), grid_spec=gr...]
  transfers between devices with their start and end apart: 9 -> 10, of which waited for: 5 -> 5; matrix products, arithmetic and copies ran while one was open for 35% -> 41% of each run, Pallas kernels for 28% -> 28%
where the time goes in v2:
time: 959 us; the launch traced here: 945 us
  Pallas kernels  268 us (28%)
  matrix products  231 us (24%)
  waiting for transfers between devices  218 us (23%)
  other arithmetic  119 us (12%)
  blocking collectives  47.6 us (5%)
  local copies, waits for them, and re-layouts  46.4 us (5%)
  between operations  14.4 us (2%)
    pallas_call x3, Pallas kernels, expert_partials(): pl.pallas_call(functools.partial(expert_kernel, first_part), grid_spec=gr...  268 us
    reduce_scatter x3, waiting for transfers between devices, local_layer(): lax.psum_scatter(partial.reshape(-1, LANES), 'ep', scatter_dimension=0, t...  116 us
    div x1, matrix products, local_layer(): jax.nn.softmax(jnp.where(causal, scores, -1e+30), axis=-1)  72.7 us
    sort x1, other arithmetic, local_layer(): lax.sort(jnp.where(member, jnp.arange(chunk_tok, dtype=jnp.int32), chunk_...  71.9 us
    all_gather x1, waiting for transfers between devices, local_layer(): key_w = lax.all_gather(k_shard, 'ep', axis=0, tiled=True)  40 us
    all_gather x1, waiting for transfers between devices, local_layer(): shared_all = lax.all_gather(shards, 'ep', axis=0)  35 us
    dot_general x1, matrix products, local_layer(): jnp.einsum('bhqk,bkhe->bqhe', attn_probs, vals_all, preferred_element_typ...  29.1 us
    dot_general x2, matrix products, local_layer(): jnp.dot(attended[rows], out_w, preferred_element_type=jnp.float32)  28.3 us
  transfers between devices with their start and end apart: 10, of which 5 were waited for; matrix products, arithmetic and copies ran while one was open for 41% of the time, Pallas kernels for 28%

profile of v2, /device:TPU:112, one launch (start us, length us, event | category | flops | bytes accessed | tf_op | source)
XLA Modules:
  0.0 945.2 jit_solution(12362043860662589184)
XLA Ops:
  11.1 25.3 %all-gather = s32[64,1024]{1,0:T(8,128)S(1)} all-gather(s32[8,1024]{1,0:T(8,128)S(1)} %bitcast.112), channel_id=2, replica_groups=mesh['dp'=2,'ep'=8] {'ep'}, dimensions={0}, use_global_device_ids=true | all-gather | bytes 294912 | tf_op jit(solution)/shard_map/all_gather | solution.py:181
  39.1 71.9 %sort.7 = s32[4,16,2048]{2,0,1:T(4,128)} sort(s32[4,16,2048]{2,0,1:T(4,128)S(1)} %iota_select_fusion), dimensions={2}, to_apply=%region_2.3 | sort | flops 2228224 | bytes 1048576 | tf_op jit(solution)/shard_map/sort | solution.py:186
  120.8 23.1 %fusion.18 = bf16[1024,32,128]{2,0,1:T(8,128)(2,1)} fusion(bf16[2048,32,128]{2,1,0:T(8,128)(2,1)} %all-gather.13.cloned.1.call-done, bf16[1,1024,2048]{2,1,0:T(8,128)(2,1)} %fusion.16), kind=kOutput, calls=%fused_computation.23 | convolution fusion | flops 17184063488 | bytes 29360128 | tf_op jit(solution)/shard_map/bsd,dhe->bshe/dot_general | solution.py:189
  143.8 40.0 %all-gather.15.cloned.1.call-done = bf16[2048,32,128]{2,1,0:T(8,128)(2,1)} async-done(((bf16[256,32,128]{2,1,0:T(8,128)(2,1)}), bf16[2048,32,128]{2,1,0:T(8,128)(2,1)}) %all-gather.15.cloned.1.call-update) | async-done | bytes 16777232 | tf_op jit(solution)/shard_map/all_gather | solution.py:176
  183.9 23.1 %fusion.21 = bf16[1024,32,128]{2,0,1:T(8,128)(2,1)} fusion(bf16[2048,32,128]{2,1,0:T(8,128)(2,1)} %all-gather.15.cloned.1.call-done, bf16[1,1024,2048]{2,1,0:T(8,128)(2,1)} %fusion.16), kind=kOutput, calls=%fused_computation.24 | convolution fusion | flops 17184063488 | bytes 29360128 | tf_op jit(solution)/shard_map/bsd,dhe->bshe/dot_general | solution.py:191
  207.0 72.7 %fusion.7 = bf16[1,32,1024,1024]{2,3,1,0:T(8,128)(2,1)} fusion(pred[1024,1024]{0,1:T(8,128)(4,1)S(1)} %iota_compare_fusion, bf16[1024,32,128]{2,0,1:T(8,128)(2,1)} %fusion.18, bf16[1024,32,128]{2,0,1:T(8,128)(2,1)} %fusion.21), kind=kOutput, calls=%fused_computation.10 | convolution fusion | flops 8757774336 | bytes 84934656 | tf_op jit(solution)/shard_map/div | solution.py:194
  279.6 23.0 %convert_bitcast_fusion = bf16[1,1024,32,128]{3,1,2,0:T(8,128)(2,1)} fusion(bf16[2048,32,128]{2,0,1:T(8,128)(2,1)} %all-gather.17.cloned.1.call-done, bf16[1,1024,2048]{2,1,0:T(8,128)(2,1)} %fusion.16), kind=kOutput, calls=%fused_computation.22 | convolution fusion | flops 17184063488 | bytes 29360128 | tf_op jit(solution)/shard_map/bsd,dhe->bshe/dot_general | solution.py:196
  302.8 29.1 %fusion.24 = bf16[32,128,1024]{2,1,0:T(8,128)(2,1)} fusion(bf16[1,32,1024,1024]{2,3,1,0:T(8,128)(2,1)} %fusion.7, bf16[1,1024,32,128]{3,1,2,0:T(8,128)(2,1)} %convert_bitcast_fusion), kind=kOutput, calls=%fused_computation.25 | convolution fusion | flops 8594128896 | bytes 83886080 | tf_op jit(solution)/shard_map/bhqk,bkhe->bqhe/dot_general | solution.py:201
  336.5 13.7 %all-gather.19.cloned.1.call-done = bf16[4096,2048]{1,0:T(8,128)(2,1)} async-done(((bf16[512,2048]{1,0:T(8,128)(2,1)}), bf16[4096,2048]{1,0:T(8,128)(2,1)}) %all-gather.19.cloned.1.call-update) | async-done | bytes 16777232 | tf_op jit(solution)/shard_map/all_gather | solution.py:178
  350.2 13.9 %fusion.39 = bf16[512,2048]{1,0:T(8,128)(2,1)S(1)} fusion(bf16[512,4096]{0,1:T(8,128)(2,1)} %bitcast.103, bf16[4096,2048]{1,0:T(8,128)(2,1)} %all-gather.19.cloned.1.call-done, bf16[1,1024,2048]{2,1,0:T(8,128)(2,1)} %param.13), kind=kOutput, calls=%fused_computation.47 | convolution fusion | flops 8595177472 | bytes 25165824 | tf_op jit(solution)/shard_map/dot_general | solution.py:209
  367.1 35.0 %all-gather.21.cloned.1.call-done = bf16[6144,768]{1,0:T(8,128)(2,1)} async-done(((bf16[768,768]{1,0:T(8,128)(2,1)}), bf16[6144,768]{1,0:T(8,128)(2,1)}) %all-gather.21.cloned.1.call-update) | async-done | bytes 9437200 | tf_op jit(solution)/shard_map/all_gather | solution.py:200
  402.3 14.3 %fusion.38 = bf16[512,2048]{1,0:T(8,128)(2,1)S(1)} fusion(bf16[4096,2048]{1,0:T(8,128)(2,1)} %all-gather.19.cloned.1.call-done, bf16[1024,4096]{0,1:T(8,128)(2,1)} %bitcast.98, bf16[1,1024,2048]{2,1,0:T(8,128)(2,1)} %param.13), kind=kOutput, calls=%fused_computation.45 | convolution fusion | flops 8595177472 | bytes 25165824 | tf_op jit(solution)/shard_map/dot_general | solution.py:209
  429.4 8.4 select_reduce_fusion
  441.5 8.2 select_reduce_fusion.1
  450.1 22.4 %all-gather.1 = f32[64,1024]{1,0:T(8,128)S(1)} all-gather(f32[8,1024]{1,0:T(8,128)S(1)} %maximum_bitcast_fusion.1), channel_id=3, replica_groups=mesh['dp'=2,'ep'=8] {'ep'}, dimensions={0}, use_global_device_ids=true | all-gather | bytes 294912 | tf_op jit(solution)/shard_map/all_gather | solution.py:226
  475.5 11.0 %all-gather.23.cloned.1.call-done = bf16[4096,16,128]{2,1,0:T(8,128)(2,1)} async-done(((bf16[512,16,128]{2,1,0:T(8,128)(2,1)}), bf16[4096,16,128]{2,1,0:T(8,128)(2,1)}) %all-gather.23.cloned.1.call-update) | async-done | bytes 16777232 | tf_op jit(solution)/shard_map/all_gather | solution.py:217
  486.5 68.1 %routed_experts.4 = f32[8,4096,128]{2,1,0:T(8,128)} custom-call(s32[16]{0:T(128)} %get-tuple-element.30.count_ref, s32[1,16,1,2048]{3,2,1,0:T(1,128)} %get-tuple-element.39.token_ref, f32[1,16,1,2176]{3,2,1,0:T(1,128)} %get-tuple-element.37.gate_ref, bf16[8,512,16,128]{3,2,1,0:T(8,128)(2,1)} %bitcast.95, bf16[16,2048,768]{2,1,0:T(8,128)(2,1)} %gate_w.5, ...), custom_call_target="tpu_custom_call" | custom-call | flops 19327352832 | bytes 176160768 | tf_op jit(solution)/shard_map/routed_experts/pallas_call | solution.py:152
  554.8 67.9 %routed_experts.3 = f32[8,4096,128]{2,1,0:T(8,128)} custom-call(s32[16]{0:T(128)} %get-tuple-element.29.count_ref, s32[1,16,1,2048]{3,2,1,0:T(1,128)} %get-tuple-element.38.token_ref, f32[1,16,1,2176]{3,2,1,0:T(1,128)} %get-tuple-element.36.gate_ref, bf16[8,512,16,128]{3,2,1,0:T(8,128)(2,1)} %bitcast.96, bf16[16,2048,768]{2,1,0:T(8,128)(2,1)} %gate_w.5, ...), custom_call_target="tpu_custom_call" | custom-call | flops 19327352832 | bytes 176160768 | tf_op jit(solution)/shard_map/routed_experts/pallas_call | solution.py:152
  626.5 132.2 %routed_experts.5 = f32[8,8192,128]{2,1,0:T(8,128)} custom-call(s32[32]{0:T(128)} %reshape.189.count_ref, s32[2,16,1,2048]{3,2,1,0:T(1,128)} %broadcast_in_dim.86.token_ref, f32[2,16,1,2176]{3,2,1,0:T(1,128)} %pad_slice_fusion.gate_ref, bf16[8,512,16,128]{3,2,1,0:T(8,128)(2,1)} %bitcast.99, bf16[16,2048,768]{2,1,0:T(8,128)(2,1)} %gate_w.5, ...), custom_call_target="tpu_custom_call" | custom-call | flops 38654705664 | bytes 352321536 | tf_op jit(solution)/shard_map/routed_experts/pallas_call | solution.py:152
  764.4 6.7 fusion.64
  771.1 6.8 reshape.185
  778.0 8.4 fusion.48
  786.3 14.5 %convolution_convert_fusion = bf16[1024,2048]{1,0:T(8,128)(2,1)} fusion(bf16[768,2048]{1,0:T(8,128)(2,1)} %reshape.185, f32[1024,768]{1,0:T(8,128)} %fusion.48, bf16[2048,768]{1,0:T(8,128)(2,1)} %bitcast.104, bf16[512,2048]{1,0:T(8,128)(2,1)} %fusion.31, bf16[512,2048]{1,0:T(8,128)(2,1)} %fusion.29), kind=kOutput, calls=%fused_computation.54 | convolution fusion | flops 6457655296 | bytes 17825792 | tf_op jit(solution)/shard_map/dot_general | solution.py:238
  811.1 115.7 %reduce-scatter.8.cloned.1.call-done = f32[8192,128]{1,0:T(8,128)} async-done(((f32[65536,128]{1,0:T(8,128)}), f32[8192,128]{1,0:T(8,128)}) %reduce-scatter.8.cloned.1.call-update) | async-done | bytes 4194320 | tf_op jit(solution)/shard_map/reduce_scatter | solution.py:247
  (127 shorter events, 75.4 us)
Async XLA Ops:
  6.5 114.2 %all-gather.13.cloned.1.call-start = ((), (), s32[]{:S(2)}) async-start(), calls=%async_computation.3 | async-start | bytes 18874368 | tf_op jit(solution)/shard_map/all_gather | solution.py:175
  7.3 176.5 %all-gather.15.cloned.1.call-start = ((), (), s32[]{:S(2)}) async-start(), calls=%async_computation.4 | async-start | bytes 18874368 | tf_op jit(solution)/shard_map/all_gather | solution.py:176
  8.1 271.5 %all-gather.17.cloned.1.call-start = ((), (), s32[]{:S(2)}) async-start(), calls=%async_computation.5 | async-start | bytes 18874368 | tf_op jit(solution)/shard_map/all_gather | solution.py:177
  10.4 339.9 %all-gather.19.cloned.1.call-start = ((), (), s32[]{:S(2)}) async-start(), calls=%async_computation.6 | async-start | bytes 18874368 | tf_op jit(solution)/shard_map/all_gather | solution.py:178
  11.0 391.1 %all-gather.21.cloned.1.call-start = ((), (), s32[]{:S(2)}) async-start(), calls=%async_computation.10 | async-start | bytes 10616832 | tf_op jit(solution)/shard_map/all_gather | solution.py:200
  111.1 4.9 copy-start.4
  116.0 3.2 copy-start.11
  116.0 3.2 copy-start.12
  302.7 183.8 %all-gather.23.cloned.1.call-start = ((), (), s32[]{:S(2)}) async-start(), calls=%async_computation.11 | async-start | bytes 18874368 | tf_op jit(solution)/shard_map/all_gather | solution.py:217
  364.2 73.8 %copy-start = (bf16[512,2048]{1,0:T(8,128)(2,1)}, bf16[512,2048]{1,0:T(8,128)(2,1)S(1)}, u32[]{:S(2)}) copy-start(bf16[512,2048]{1,0:T(8,128)(2,1)S(1)} %fusion.39) | copy-start | bytes 6291460
  364.7 73.3 %copy-start.17 = (f32[512]{0:T(512)}, f32[512]{0:T(512)S(1)}, u32[]{:S(2)}) copy-start(f32[512]{0:T(512)S(1)} %add_rsqrt_fusion.2) | copy-start | bytes 6148
  402.2 224.3 %all-gather.25.cloned.1.call-start = ((), (), s32[]{:S(2)}) async-start(), calls=%async_computation.12 | async-start | bytes 18874368 | tf_op jit(solution)/shard_map/all_gather | solution.py:217
  417.1 7.2 copy-start.19
  417.6 3.8 copy-start.16
  417.6 6.7 copy-start.5
  419.7 381.2 %reduce-scatter.6.cloned.1.call-start = ((), (), s32[]{:S(2)}) async-start(), calls=%async_computation.8 | async-start | bytes 18874368 | tf_op jit(solution)/shard_map/reduce_scatter | solution.py:247
  424.3 48.1 %copy-start.22 = (s32[16]{0:T(128)S(1)}, s32[16]{0:T(128)}, u32[]{:S(2)}) copy-start(s32[16]{0:T(128)} %copy-done.21) | copy-start | bytes 196
  438.0 34.4 %copy-start.9 = (s32[64,1024]{1,0:T(8,128)S(1)}, s32[64,1024]{1,0:T(8,128)}, u32[]{:S(2)}) copy-start(s32[64,1024]{1,0:T(8,128)} %copy-done.8) | copy-start | bytes 786436
  554.7 248.8 %reduce-scatter.4.cloned.1.call-start = ((), (), s32[]{:S(2)}) async-start(), calls=%async_computation.7 | async-start | bytes 18874368 | tf_op jit(solution)/shard_map/reduce_scatter | solution.py:247
  622.8 304.1 %reduce-scatter.8.cloned.1.call-start = ((), (), s32[]{:S(2)}) async-start(), calls=%async_computation.9 | async-start | bytes 37748736 | tf_op jit(solution)/shard_map/reduce_scatter | solution.py:247
  759.3 3.4 copy-start.1
  759.3 3.4 copy-start.18
  811.1 120.6 %copy-start.3 = (bf16[512,2048]{1,0:T(8,128)(2,1)S(1)}, bf16[512,2048]{1,0:T(8,128)(2,1)}, u32[]{:S(2)}) copy-start(bf16[512,2048]{1,0:T(8,128)(2,1)} %copy-done.2) | copy-start | bytes 6291460
  931.7 3.9 copy-start.6
  (9 other events, 17.3 us)
Sparse Core Ops, SparseCore 0:
  9.0 85.6 all-gather.12
  96.3 87.5 all-gather.14
  185.4 81.6 all-gather.16
  268.6 81.6 all-gather.18
  351.7 50.4 all-gather.20
  403.6 82.9 all-gather.22
  488.1 81.6 all-gather.24
  572.2 88.2 reduce-scatter.5
  662.8 87.3 reduce-scatter.3
  758.8 167.9 reduce-scatter.7
